TPU v7x, 32 devices: a whole 2x2x4 slice. The times are simulated.
32 devices in a mesh: rep: 16 (over z, y, x), dom: 2 (over core).
Axes of the slice: x: 2, y: 2, z: 4, core: 2. Of those that a mesh axis runs over, the one named last changes fastest.
Arguments:
- protein_pos: float32 [3, 65536], P(None, ('rep', 'dom')), parts along dimension 1, may hold values from -4 to 4, as said below
- protein_vel: float32 [3, 65536], P(None, ('rep', 'dom')), parts along dimension 1, may hold values from -3 to 3
- inv_mass: float32 [65536], P(('rep', 'dom')), parts along dimension 0, may hold values from 0.0625 to 1
- bond_atoms: int32 [2, 40960], P(None, ('rep', 'dom')), parts along dimension 1, may hold values from 0 to 2047, as said below
- left_atoms: int32 [12288], P(('rep', 'dom')), parts along dimension 0, may hold values from 0 to 2047, as said below
- right_atoms: int32 [12288], P(('rep', 'dom')), parts along dimension 0, may hold values from 0 to 2047, as said below
- water_pos: float32 [9, 32768], P(None, ('rep', 'dom')), parts along dimension 1, may hold values from -3.2 to 3.2, as said below
- water_vel: float32 [9, 32768], P(None, ('rep', 'dom')), parts along dimension 1, may hold values from -3 to 3
Outputs:
- protein_velocity: float32 [3, 65536], P(None, ('rep', 'dom')), parts along dimension 1
- water_velocity: float32 [9, 32768], P(None, ('rep', 'dom')), parts along dimension 1
There are 16 independent parts, one for each index of `rep`. A program takes and returns all parts, laid end to end along the dimension named above; each array names one. Nothing has to cross between parts.
Inputs may be any that keep to these rules, and one draw needn't show every extreme that they name: `bond_atoms`: indices within the domain's block of 2048 atoms; each column joins two different atoms; together with the cross bonds the bonds form a forest. `left_atoms`: distinct indices within the domain's block, none of them in right_atoms. `right_atoms`: distinct indices within the domain's block. `protein_pos`: every bond and every cross bond joins atoms 0.1 to 0.15 apart. `water_pos`: each column holds one rigid water: oxygen, then two hydrogens, 0.09572 from the oxygen and 0.15139 from each other.
All inputs are finite; a program needn't handle non-finite values.
Results may differ from a plain program's by a relative error of at most 0.0003.
Values sent between devices are 32-bit elements; how exact they have to be, the bound alone decides.
A program may use at most 64 MiB of HBM per device.

v0:
```python
import math

import jax
import jax.numpy as jnp
from jax import lax
from jax.sharding import PartitionSpec as P

ORDER = 4
ITER = 2


time_step = 0.002
mass_oxygen = 15.9994
mass_hydrogen = 1.008
oxygen_hydrogen = 0.09572
hydrogen_pair = 0.15139
total_mass = mass_oxygen + 2.0 * mass_hydrogen
half_pair = 0.5 * hydrogen_pair
water_height = math.sqrt(oxygen_hydrogen * oxygen_hydrogen - half_pair * half_pair)
oxygen_reach = 2.0 * mass_hydrogen * water_height / total_mass
hydrogen_reach = water_height - oxygen_reach


def shifted(value, axis, steps):
    count = lax.axis_size(axis)
    pairs = [(source, (source + steps) % count) for source in range(count)]
    return lax.ppermute(value, axis, pairs)


def cross_product(left, right):
    return jnp.stack(
        [
            left[1] * right[2] - left[2] * right[1],
            left[2] * right[0] - left[0] * right[2],
            left[0] * right[1] - left[1] * right[0],
        ]
    )


def inner(left, right):
    return jnp.sum(left * right, axis=0)


def settle(before, after):
    old_oxygen, old_first, old_second = (before[0:3], before[3:6], before[6:9])
    new_oxygen, new_first, new_second = (after[0:3], after[3:6], after[6:9])
    center = (mass_oxygen * new_oxygen + mass_hydrogen * (new_first + new_second)) / total_mass
    old_b = old_first - old_oxygen
    old_c = old_second - old_oxygen
    rel_a = new_oxygen - center
    rel_b = new_first - center
    rel_c = new_second - center
    normal = cross_product(old_b, old_c)
    side = cross_product(rel_a, normal)
    upward = cross_product(normal, side)
    axis_z = normal / jnp.sqrt(inner(normal, normal))
    axis_x = side / jnp.sqrt(inner(side, side))
    axis_y = upward / jnp.sqrt(inner(upward, upward))
    oldb_x = inner(axis_x, old_b)
    oldb_y = inner(axis_y, old_b)
    oldc_x = inner(axis_x, old_c)
    oldc_y = inner(axis_y, old_c)
    newa_z = inner(axis_z, rel_a)
    newb_x = inner(axis_x, rel_b)
    newb_y = inner(axis_y, rel_b)
    newb_z = inner(axis_z, rel_b)
    newc_x = inner(axis_x, rel_c)
    newc_y = inner(axis_y, rel_c)
    newc_z = inner(axis_z, rel_c)
    sin_phi = newa_z / oxygen_reach
    cos_phi = jnp.sqrt(1.0 - sin_phi * sin_phi)
    sin_psi = (newb_z - newc_z) / (2.0 * half_pair * cos_phi)
    cos_psi = jnp.sqrt(1.0 - sin_psi * sin_psi)
    rest_ay = oxygen_reach * cos_phi
    rest_bx = -half_pair * cos_psi
    lowered = -hydrogen_reach * cos_phi
    tilted = half_pair * sin_psi * sin_phi
    rest_by = lowered - tilted
    rest_cy = lowered + tilted
    alpha = rest_bx * (oldb_x - oldc_x) + oldb_y * rest_by + oldc_y * rest_cy
    beta = rest_bx * (oldc_y - oldb_y) + oldb_x * rest_by + oldc_x * rest_cy
    gamma = oldb_x * newb_y - newb_x * oldb_y + oldc_x * newc_y - newc_x * oldc_y
    summed = alpha * alpha + beta * beta
    sin_theta = (alpha * gamma - beta * jnp.sqrt(summed - gamma * gamma)) / summed
    cos_theta = jnp.sqrt(1.0 - sin_theta * sin_theta)
    final_ax = -rest_ay * sin_theta
    final_ay = rest_ay * cos_theta
    final_bx = rest_bx * cos_theta - rest_by * sin_theta
    final_by = rest_bx * sin_theta + rest_by * cos_theta
    final_cx = -rest_bx * cos_theta - rest_cy * sin_theta
    final_cy = -rest_bx * sin_theta + rest_cy * cos_theta
    oxygen = center + axis_x * final_ax + axis_y * final_ay + axis_z * newa_z
    first = center + axis_x * final_bx + axis_y * final_by + axis_z * newb_z
    second = center + axis_x * final_cx + axis_y * final_cy + axis_z * newc_z
    return jnp.concatenate([oxygen, first, second], axis=0)


def solve_bonds(old_ext, moved_ext, mass_ext, first, second, count, atom_field):
    diff = old_ext[:, first] - old_ext[:, second]
    length = jnp.sqrt(inner(diff, diff))
    unit = diff / length
    scale = 1.0 / jnp.sqrt(mass_ext[first] + mass_ext[second])
    delta = jnp.zeros_like(moved_ext)
    rhs = scale * (inner(unit, moved_ext[:, first] - moved_ext[:, second]) - length)
    for round_index in range(ITER + 1):
        if round_index > 0:
            now = moved_ext + delta
            gap = now[:, first] - now[:, second]
            target = jnp.sqrt(2.0 * length * length - inner(gap, gap))
            rhs = scale * (length - target)
        total = rhs
        current = rhs
        for order_index in range(ORDER):
            field = atom_field(unit * (scale * current), True)
            current = current - scale * inner(unit, field[:, first] - field[:, second])
            total = total + current
        if round_index == ITER:
            return delta[:, :count] - atom_field(unit * (scale * total), False)
        delta = delta - atom_field(unit * (scale * total), True)


def on_device(
    protein_pos, protein_vel, inv_mass, bond_atoms, left_atoms, right_atoms, water_pos, water_vel
):
    count = protein_pos.shape[1]
    halo = left_atoms.shape[0]
    moved = protein_pos + time_step * protein_vel
    slots = jnp.arange(halo, dtype=jnp.int32)
    cap_data = jnp.concatenate(
        [protein_pos[:, left_atoms], moved[:, left_atoms], inv_mass[left_atoms][None]], axis=0
    )
    caps = shifted(cap_data, "dom", -1)
    old_ext = jnp.concatenate([protein_pos, caps[0:3]], axis=1)
    moved_ext = jnp.concatenate([moved, caps[3:6]], axis=1)
    mass_ext = jnp.concatenate([inv_mass, caps[6]])
    first = jnp.concatenate([bond_atoms[0], right_atoms])
    second = jnp.concatenate([bond_atoms[1], count + slots])

    def atom_field(weighted, edges):
        force = (
            jnp.zeros((3, count + halo), jnp.float32)
            .at[:, first]
            .add(weighted)
            .at[:, second]
            .add(-weighted)
        )
        returned = shifted(force[:, count:], "dom", 1)
        own_field = inv_mass * force[:, :count].at[:, left_atoms].add(returned)
        if edges:
            edge_field = shifted(own_field[:, left_atoms], "dom", -1)
            return jnp.concatenate([own_field, edge_field], axis=1)
        return own_field

    water_moved = water_pos + time_step * water_vel
    settled = settle(water_pos, water_moved)
    water_velocity = water_vel + (settled - water_moved) / time_step
    delta = solve_bonds(old_ext, moved_ext, mass_ext, first, second, count, atom_field)
    protein_velocity = protein_vel + delta / time_step
    return (protein_velocity, water_velocity)


def solution(mesh):
    in_specs = (
        P(None, ("rep", "dom")),
        P(None, ("rep", "dom")),
        P(("rep", "dom")),
        P(None, ("rep", "dom")),
        P(("rep", "dom")),
        P(("rep", "dom")),
        P(None, ("rep", "dom")),
        P(None, ("rep", "dom")),
    )
    out_specs = (P(None, ("rep", "dom")), P(None, ("rep", "dom")))
    return jax.shard_map(
        on_device, mesh=mesh, in_specs=in_specs, out_specs=out_specs, check_vma=False
    )
```

profile of v0, /device:TPU:3, one launch (start us, length us, event | category | flops | bytes accessed | tf_op | source)
XLA Modules:
  0.0 701.6 jit_solution(17388607251286904742)
XLA Ops:
  8.8 9.1 %gather_fusion.6 = f32[1664]{0:T(1024)S(1)} fusion(f32[2432]{0:T(1024)S(1)} %pad_maximum_fusion.18, s32[2048]{0:T(1024)S(1)} %pad_clamp_fusion), kind=kCustom, calls=%fused_computation.6 | custom fusion | bytes 19968 | tf_op jit(solution)/shard_map/gather | solution.py:102
  17.9 9.1 %gather_fusion.5 = f32[1664]{0:T(1024)S(1)} fusion(f32[2432]{0:T(1024)S(1)} %pad_maximum_fusion.18, s32[2048]{0:T(1024)S(1)} %pad_clamp_fusion.1), kind=kCustom, calls=%fused_computation.5 | custom fusion | bytes 19968 | tf_op jit(solution)/shard_map/gather | solution.py:102
  27.3 4.2 gather_fusion.4
  31.5 4.2 gather_fusion.3
  46.8 13.0 %scatter_custom_fusion = f32[3,2432]{0,1:T(8,128)S(1)} fusion(s32[1664]{0:T(1024)S(1)} %get-tuple-element.68, f32[]{:T(128)} %constant.17.clone.1, f32[1664]{0:T(1024)S(1)} %get-tuple-element.49, f32[1664,3]{1,0:T(8,128)S(1)} %get-tuple-element.53, f32[1664]{0:T(1024)S(1)} %sqrt.199), kind=kCustom, calls=%fused_computation.185 | custom fusion | flops 14976 | bytes 897540 | tf_op jit(solution)/shard_map/scatter-add | solution.py:143
  59.7 13.3 %scatter_custom_fusion.1 = f32[3,2432]{0,1:T(8,128)S(1)} fusion(f32[3,2432]{0,1:T(8,128)S(1)} %scatter_custom_fusion, s32[1664]{0:T(1024)S(1)} %get-tuple-element.69, f32[1664]{0:T(1024)S(1)} %get-tuple-element.49, f32[1664,3]{1,0:T(8,128)S(1)} %get-tuple-element.53, f32[1664]{0:T(1024)S(1)} %sqrt.199), kind=kCustom, calls=%fused_computation.125 | custom fusion | flops 19968 | bytes 897536 | tf_op jit(solution)/shard_map/scatter-add | solution.py:145
  85.1 4.2 gather_fusion.10
  91.1 13.0 %scatter_custom_fusion.3 = f32[3,2432]{0,1:T(8,128)S(1)} fusion(s32[1664]{0:T(1024)S(1)} %get-tuple-element.68, f32[]{:T(128)} %constant.17.clone.1, f32[1664]{0:T(1024)S(1)} %fusion.163, f32[1664,3]{1,0:T(8,128)S(1)} %get-tuple-element.53, f32[1664]{0:T(1024)S(1)} %sqrt.199), kind=kCustom, calls=%fused_computation.182 | custom fusion | flops 14976 | bytes 897540 | tf_op jit(solution)/shard_map/scatter-add | solution.py:143
  104.0 13.3 %scatter_custom_fusion.4 = f32[3,2432]{0,1:T(8,128)S(1)} fusion(f32[3,2432]{0,1:T(8,128)S(1)} %scatter_custom_fusion.3, s32[1664]{0:T(1024)S(1)} %get-tuple-element.69, f32[1664]{0:T(1024)S(1)} %fusion.163, f32[1664,3]{1,0:T(8,128)S(1)} %get-tuple-element.53, f32[1664]{0:T(1024)S(1)} %sqrt.199), kind=kCustom, calls=%fused_computation.123 | custom fusion | flops 19968 | bytes 897536 | tf_op jit(solution)/shard_map/scatter-add | solution.py:145
  129.6 4.2 gather_fusion.13
  135.6 13.0 %scatter_custom_fusion.6 = f32[3,2432]{0,1:T(8,128)S(1)} fusion(s32[1664]{0:T(1024)S(1)} %get-tuple-element.68, f32[]{:T(128)} %constant.17.clone.1, f32[1664]{0:T(1024)S(1)} %fusion.167, f32[1664,3]{1,0:T(8,128)S(1)} %get-tuple-element.53, f32[1664]{0:T(1024)S(1)} %sqrt.199), kind=kCustom, calls=%fused_computation.179 | custom fusion | flops 14976 | bytes 897540 | tf_op jit(solution)/shard_map/scatter-add | solution.py:143
  148.5 13.3 %scatter_custom_fusion.7 = f32[3,2432]{0,1:T(8,128)S(1)} fusion(f32[3,2432]{0,1:T(8,128)S(1)} %scatter_custom_fusion.6, s32[1664]{0:T(1024)S(1)} %get-tuple-element.69, f32[1664]{0:T(1024)S(1)} %fusion.167, f32[1664,3]{1,0:T(8,128)S(1)} %get-tuple-element.53, f32[1664]{0:T(1024)S(1)} %sqrt.199), kind=kCustom, calls=%fused_computation.121 | custom fusion | flops 19968 | bytes 897536 | tf_op jit(solution)/shard_map/scatter-add | solution.py:145
  173.9 4.2 gather_fusion.16
  179.8 13.0 %scatter_custom_fusion.9 = f32[3,2432]{0,1:T(8,128)S(1)} fusion(s32[1664]{0:T(1024)S(1)} %get-tuple-element.68, f32[]{:T(128)} %constant.17.clone.1, f32[1664]{0:T(1024)S(1)} %fusion.158, f32[1664,3]{1,0:T(8,128)S(1)} %get-tuple-element.53, f32[1664]{0:T(1024)S(1)} %sqrt.199), kind=kCustom, calls=%fused_computation.176 | custom fusion | flops 14976 | bytes 897540 | tf_op jit(solution)/shard_map/scatter-add | solution.py:143
  192.8 13.3 %scatter_custom_fusion.10 = f32[3,2432]{0,1:T(8,128)S(1)} fusion(f32[3,2432]{0,1:T(8,128)S(1)} %scatter_custom_fusion.9, s32[1664]{0:T(1024)S(1)} %get-tuple-element.69, f32[1664]{0:T(1024)S(1)} %fusion.158, f32[1664,3]{1,0:T(8,128)S(1)} %get-tuple-element.53, f32[1664]{0:T(1024)S(1)} %sqrt.199), kind=kCustom, calls=%fused_computation.119 | custom fusion | flops 19968 | bytes 897536 | tf_op jit(solution)/shard_map/scatter-add | solution.py:145
  218.2 4.2 gather_fusion.19
  224.1 13.0 %scatter_custom_fusion.12 = f32[3,2432]{0,1:T(8,128)S(1)} fusion(s32[1664]{0:T(1024)S(1)} %get-tuple-element.68, f32[]{:T(128)} %constant.17.clone.1, f32[1664]{0:T(1024)S(1)} %add_multiply_fusion.3, f32[1664,3]{1,0:T(8,128)S(1)} %get-tuple-element.53, f32[1664]{0:T(1024)S(1)} %sqrt.199), kind=kCustom, calls=%fused_computation.173 | custom fusion | flops 14976 | bytes 897540 | tf_op jit(solution)/shard_map/scatter-add | solution.py:143
  237.1 13.3 %scatter_custom_fusion.13 = f32[3,2432]{0,1:T(8,128)S(1)} fusion(f32[3,2432]{0,1:T(8,128)S(1)} %scatter_custom_fusion.12, s32[1664]{0:T(1024)S(1)} %get-tuple-element.69, f32[1664]{0:T(1024)S(1)} %add_multiply_fusion.3, f32[1664,3]{1,0:T(8,128)S(1)} %get-tuple-element.53, f32[1664]{0:T(1024)S(1)} %sqrt.199), kind=kCustom, calls=%fused_computation.117 | custom fusion | flops 19968 | bytes 897536 | tf_op jit(solution)/shard_map/scatter-add | solution.py:145
  263.0 4.2 gather_fusion.22
  268.7 13.0 %scatter_custom_fusion.15 = f32[3,2432]{0,1:T(8,128)S(1)} fusion(s32[1664]{0:T(1024)S(1)} %get-tuple-element.68, f32[]{:T(128)} %constant.17.clone.1, f32[1664]{0:T(1024)S(1)} %get-tuple-element.47, f32[1664,3]{1,0:T(8,128)S(1)} %get-tuple-element.53, f32[1664]{0:T(1024)S(1)} %sqrt.199), kind=kCustom, calls=%fused_computation.170 | custom fusion | flops 14976 | bytes 897540 | tf_op jit(solution)/shard_map/scatter-add | solution.py:143
  281.7 13.3 %scatter_custom_fusion.16 = f32[3,2432]{0,1:T(8,128)S(1)} fusion(f32[3,2432]{0,1:T(8,128)S(1)} %scatter_custom_fusion.15, s32[1664]{0:T(1024)S(1)} %get-tuple-element.69, f32[1664]{0:T(1024)S(1)} %get-tuple-element.47, f32[1664,3]{1,0:T(8,128)S(1)} %get-tuple-element.53, f32[1664]{0:T(1024)S(1)} %sqrt.199), kind=kCustom, calls=%fused_computation.115 | custom fusion | flops 19968 | bytes 897536 | tf_op jit(solution)/shard_map/scatter-add | solution.py:145
  307.0 4.2 gather_fusion.25
  313.0 13.0 %scatter_custom_fusion.18 = f32[3,2432]{0,1:T(8,128)S(1)} fusion(s32[1664]{0:T(1024)S(1)} %get-tuple-element.68, f32[]{:T(128)} %constant.17.clone.1, f32[1664]{0:T(1024)S(1)} %fusion.164, f32[1664,3]{1,0:T(8,128)S(1)} %get-tuple-element.53, f32[1664]{0:T(1024)S(1)} %sqrt.199), kind=kCustom, calls=%fused_computation.167 | custom fusion | flops 14976 | bytes 897540 | tf_op jit(solution)/shard_map/scatter-add | solution.py:143
  325.9 13.3 %scatter_custom_fusion.19 = f32[3,2432]{0,1:T(8,128)S(1)} fusion(f32[3,2432]{0,1:T(8,128)S(1)} %scatter_custom_fusion.18, s32[1664]{0:T(1024)S(1)} %get-tuple-element.69, f32[1664]{0:T(1024)S(1)} %fusion.164, f32[1664,3]{1,0:T(8,128)S(1)} %get-tuple-element.53, f32[1664]{0:T(1024)S(1)} %sqrt.199), kind=kCustom, calls=%fused_computation.113 | custom fusion | flops 19968 | bytes 897536 | tf_op jit(solution)/shard_map/scatter-add | solution.py:145
  351.3 4.2 gather_fusion.28
  357.3 13.0 %scatter_custom_fusion.21 = f32[3,2432]{0,1:T(8,128)S(1)} fusion(s32[1664]{0:T(1024)S(1)} %get-tuple-element.68, f32[]{:T(128)} %constant.17.clone.1, f32[1664]{0:T(1024)S(1)} %fusion.168, f32[1664,3]{1,0:T(8,128)S(1)} %get-tuple-element.53, f32[1664]{0:T(1024)S(1)} %sqrt.199), kind=kCustom, calls=%fused_computation.164 | custom fusion | flops 14976 | bytes 897540 | tf_op jit(solution)/shard_map/scatter-add | solution.py:143
  370.2 13.3 %scatter_custom_fusion.22 = f32[3,2432]{0,1:T(8,128)S(1)} fusion(f32[3,2432]{0,1:T(8,128)S(1)} %scatter_custom_fusion.21, s32[1664]{0:T(1024)S(1)} %get-tuple-element.69, f32[1664]{0:T(1024)S(1)} %fusion.168, f32[1664,3]{1,0:T(8,128)S(1)} %get-tuple-element.53, f32[1664]{0:T(1024)S(1)} %sqrt.199), kind=kCustom, calls=%fused_computation.111 | custom fusion | flops 19968 | bytes 897536 | tf_op jit(solution)/shard_map/scatter-add | solution.py:145
  395.8 4.2 gather_fusion.31
  401.8 13.0 %scatter_custom_fusion.24 = f32[3,2432]{0,1:T(8,128)S(1)} fusion(s32[1664]{0:T(1024)S(1)} %get-tuple-element.68, f32[]{:T(128)} %constant.17.clone.1, f32[1664]{0:T(1024)S(1)} %fusion.159, f32[1664,3]{1,0:T(8,128)S(1)} %get-tuple-element.53, f32[1664]{0:T(1024)S(1)} %sqrt.199), kind=kCustom, calls=%fused_computation.161 | custom fusion | flops 14976 | bytes 897540 | tf_op jit(solution)/shard_map/scatter-add | solution.py:143
  414.7 13.3 %scatter_custom_fusion.25 = f32[3,2432]{0,1:T(8,128)S(1)} fusion(f32[3,2432]{0,1:T(8,128)S(1)} %scatter_custom_fusion.24, s32[1664]{0:T(1024)S(1)} %get-tuple-element.69, f32[1664]{0:T(1024)S(1)} %fusion.159, f32[1664,3]{1,0:T(8,128)S(1)} %get-tuple-element.53, f32[1664]{0:T(1024)S(1)} %sqrt.199), kind=kCustom, calls=%fused_computation.109 | custom fusion | flops 19968 | bytes 897536 | tf_op jit(solution)/shard_map/scatter-add | solution.py:145
  440.1 4.2 gather_fusion.34
  446.0 13.0 %scatter_custom_fusion.27 = f32[3,2432]{0,1:T(8,128)S(1)} fusion(s32[1664]{0:T(1024)S(1)} %get-tuple-element.68, f32[]{:T(128)} %constant.17.clone.1, f32[1664]{0:T(1024)S(1)} %add_multiply_fusion.2, f32[1664,3]{1,0:T(8,128)S(1)} %get-tuple-element.53, f32[1664]{0:T(1024)S(1)} %sqrt.199), kind=kCustom, calls=%fused_computation.158 | custom fusion | flops 14976 | bytes 897540 | tf_op jit(solution)/shard_map/scatter-add | solution.py:143
  459.0 13.3 %scatter_custom_fusion.28 = f32[3,2432]{0,1:T(8,128)S(1)} fusion(f32[3,2432]{0,1:T(8,128)S(1)} %scatter_custom_fusion.27, s32[1664]{0:T(1024)S(1)} %get-tuple-element.69, f32[1664]{0:T(1024)S(1)} %add_multiply_fusion.2, f32[1664,3]{1,0:T(8,128)S(1)} %get-tuple-element.53, f32[1664]{0:T(1024)S(1)} %sqrt.199), kind=kCustom, calls=%fused_computation.107 | custom fusion | flops 19968 | bytes 897536 | tf_op jit(solution)/shard_map/scatter-add | solution.py:145
  484.5 4.2 gather_fusion.37
  490.1 13.1 %scatter_custom_fusion.30 = f32[3,2432]{0,1:T(8,128)S(1)} fusion(s32[1664]{0:T(1024)} %copy-done.31, f32[]{:T(128)} %constant.17.clone.1, f32[1664]{0:T(1024)S(1)} %get-tuple-element.43, f32[1664,3]{1,0:T(8,128)S(1)} %get-tuple-element.53, f32[1664]{0:T(1024)S(1)} %sqrt.199), kind=kCustom, calls=%fused_computation.155 | custom fusion | flops 14976 | bytes 62976 | tf_op jit(solution)/shard_map/scatter-add | solution.py:143
  503.3 13.4 %scatter_custom_fusion.31 = f32[3,2432]{0,1:T(8,128)S(1)} fusion(f32[3,2432]{0,1:T(8,128)S(1)} %scatter_custom_fusion.30, s32[1664]{0:T(1024)} %copy-done.30, f32[1664]{0:T(1024)S(1)} %get-tuple-element.43, f32[1664,3]{1,0:T(8,128)S(1)} %get-tuple-element.53, f32[1664]{0:T(1024)S(1)} %sqrt.199), kind=kCustom, calls=%fused_computation.105 | custom fusion | flops 19968 | bytes 897536 | tf_op jit(solution)/shard_map/scatter-add | solution.py:145
  529.0 4.2 gather_fusion.40
  534.9 13.1 %scatter_custom_fusion.33 = f32[3,2432]{0,1:T(8,128)S(1)} fusion(s32[1664]{0:T(1024)} %copy-done.31, f32[]{:T(128)} %constant.17.clone.1, f32[1664]{0:T(1024)S(1)} %fusion.165, f32[1664,3]{1,0:T(8,128)S(1)} %get-tuple-element.53, f32[1664]{0:T(1024)S(1)} %sqrt.199), kind=kCustom, calls=%fused_computation.152 | custom fusion | flops 14976 | bytes 62976 | tf_op jit(solution)/shard_map/scatter-add | solution.py:143
  548.0 13.4 %scatter_custom_fusion.34 = f32[3,2432]{0,1:T(8,128)S(1)} fusion(f32[3,2432]{0,1:T(8,128)S(1)} %scatter_custom_fusion.33, s32[1664]{0:T(1024)} %copy-done.30, f32[1664]{0:T(1024)S(1)} %fusion.165, f32[1664,3]{1,0:T(8,128)S(1)} %get-tuple-element.53, f32[1664]{0:T(1024)S(1)} %sqrt.199), kind=kCustom, calls=%fused_computation.103 | custom fusion | flops 19968 | bytes 897536 | tf_op jit(solution)/shard_map/scatter-add | solution.py:145
  573.5 4.2 gather_fusion.43
  579.4 13.1 %scatter_custom_fusion.36 = f32[3,2432]{0,1:T(8,128)S(1)} fusion(s32[1664]{0:T(1024)} %copy-done.31, f32[]{:T(128)} %constant.17.clone.1, f32[1664]{0:T(1024)S(1)} %fusion.169, f32[1664,3]{1,0:T(8,128)S(1)} %get-tuple-element.53, f32[1664]{0:T(1024)S(1)} %sqrt.199), kind=kCustom, calls=%fused_computation.149 | custom fusion | flops 14976 | bytes 62976 | tf_op jit(solution)/shard_map/scatter-add | solution.py:143
  592.6 13.4 %scatter_custom_fusion.37 = f32[3,2432]{0,1:T(8,128)S(1)} fusion(f32[3,2432]{0,1:T(8,128)S(1)} %scatter_custom_fusion.36, s32[1664]{0:T(1024)} %copy-done.30, f32[1664]{0:T(1024)S(1)} %fusion.169, f32[1664,3]{1,0:T(8,128)S(1)} %get-tuple-element.53, f32[1664]{0:T(1024)S(1)} %sqrt.199), kind=kCustom, calls=%fused_computation.101 | custom fusion | flops 19968 | bytes 897536 | tf_op jit(solution)/shard_map/scatter-add | solution.py:145
  618.4 4.2 gather_fusion.46
  624.3 13.1 %scatter_custom_fusion.39 = f32[3,2432]{0,1:T(8,128)S(1)} fusion(s32[1664]{0:T(1024)} %copy-done.31, f32[]{:T(128)} %constant.17.clone.1, f32[1664]{0:T(1024)S(1)} %fusion.160, f32[1664,3]{1,0:T(8,128)S(1)} %get-tuple-element.53, f32[1664]{0:T(1024)S(1)} %sqrt.199), kind=kCustom, calls=%fused_computation.146 | custom fusion | flops 14976 | bytes 62976 | tf_op jit(solution)/shard_map/scatter-add | solution.py:143
  637.4 13.4 %scatter_custom_fusion.40 = f32[3,2432]{0,1:T(8,128)S(1)} fusion(f32[3,2432]{0,1:T(8,128)S(1)} %scatter_custom_fusion.39, s32[1664]{0:T(1024)} %copy-done.30, f32[1664]{0:T(1024)S(1)} %fusion.160, f32[1664,3]{1,0:T(8,128)S(1)} %get-tuple-element.53, f32[1664]{0:T(1024)S(1)} %sqrt.199), kind=kCustom, calls=%fused_computation.99 | custom fusion | flops 19968 | bytes 897536 | tf_op jit(solution)/shard_map/scatter-add | solution.py:145
  663.0 4.2 gather_fusion.49
  669.0 13.1 %scatter_custom_fusion.42 = f32[3,2432]{0,1:T(8,128)S(1)} fusion(s32[1664]{0:T(1024)} %copy-done.31, f32[]{:T(128)} %constant.17.clone.1, f32[1664]{0:T(1024)S(1)} %add_multiply_fusion.1, f32[1664,3]{1,0:T(8,128)S(1)} %get-tuple-element.53, f32[1664]{0:T(1024)S(1)} %sqrt.199), kind=kCustom, calls=%fused_computation.143 | custom fusion | flops 14976 | bytes 62976 | tf_op jit(solution)/shard_map/scatter-add | solution.py:143
  682.1 13.4 %scatter_custom_fusion.43 = f32[3,2432]{0,1:T(8,128)S(1)} fusion(f32[3,2432]{0,1:T(8,128)S(1)} %scatter_custom_fusion.42, s32[1664]{0:T(1024)} %copy-done.30, f32[1664]{0:T(1024)S(1)} %add_multiply_fusion.1, f32[1664,3]{1,0:T(8,128)S(1)} %get-tuple-element.53, f32[1664]{0:T(1024)S(1)} %sqrt.199), kind=kCustom, calls=%fused_computation.97 | custom fusion | flops 19968 | bytes 897536 | tf_op jit(solution)/shard_map/scatter-add | solution.py:145
  (387 shorter events, 218.7 us)
Async XLA Ops:
  0.6 3.3 copy-start.6
  1.3 517.0 %copy-start.44 = (s32[384]{0:T(512)}, s32[384]{0:T(512)S(1)}, u32[]{:S(2)}) copy-start(s32[384]{0:T(512)S(1)} %compare_select_fusion.2) | copy-start | bytes 4612
  3.9 4.0 copy-start.45
  4.0 4.0 copy-start.43
  7.2 1.6 collective-permute-start
  8.1 437.9 %copy-start.31 = (s32[1664]{0:T(1024)}, s32[1664]{0:T(1024)S(1)}, u32[]{:S(2)}) copy-start(s32[1664]{0:T(1024)S(1)} %get-tuple-element.68) | copy-start | bytes 19972
  8.1 450.9 %copy-start.30 = (s32[1664]{0:T(1024)}, s32[1664]{0:T(1024)S(1)}, u32[]{:S(2)}) copy-start(s32[1664]{0:T(1024)S(1)} %get-tuple-element.69) | copy-start | bytes 19972
  35.6 8.8 %copy-start.1 = (f32[1664,3]{1,0:T(8,128)S(1)}, f32[1664,3]{1,0:T(8,128)}, u32[]{:S(2)}) copy-start(f32[1664,3]{1,0:T(8,128)} %gather_fusion.4) | copy-start | bytes 59908
  73.0 1.6 collective-permute-start.1
  80.2 1.2 collective-permute-start.2
  117.3 1.6 collective-permute-start.3
  124.7 1.2 collective-permute-start.4
  161.8 1.6 collective-permute-start.5
  169.0 1.2 collective-permute-start.6
  206.1 1.6 collective-permute-start.7
  213.3 1.2 collective-permute-start.8
  250.4 1.6 collective-permute-start.9
  257.7 1.5 collective-permute-start.10
  259.3 7.9 %copy-start.22 = (f32[3,384]{1,0:T(4,128)}, f32[3,384]{1,0:T(4,128)S(1)}, u32[]{:S(2)}) copy-start(f32[3,384]{1,0:T(4,128)S(1)} %copy.161) | copy-start | bytes 13828
  295.0 1.6 collective-permute-start.11
  302.1 1.2 collective-permute-start.12
  339.2 1.6 collective-permute-start.13
  346.4 1.2 collective-permute-start.14
  383.5 1.6 collective-permute-start.15
  390.9 1.2 collective-permute-start.16
  428.0 1.6 collective-permute-start.17
  435.2 1.2 collective-permute-start.18
  459.0 13.7 %copy-start.4 = (f32[9,1024]{1,0:T(8,128)S(1)}, f32[9,1024]{1,0:T(8,128)}, u32[]{:S(2)}) copy-start(f32[9,1024]{1,0:T(8,128)} %param.14) | copy-start | bytes 110596
  459.0 13.7 %copy-start.5 = (f32[9,1024]{1,0:T(8,128)S(1)}, f32[9,1024]{1,0:T(8,128)}, u32[]{:S(2)}) copy-start(f32[9,1024]{1,0:T(8,128)} %param.15) | copy-start | bytes 110596
  472.3 1.6 collective-permute-start.19
  479.5 1.2 collective-permute-start.20
  516.7 1.6 collective-permute-start.21
  524.1 1.2 collective-permute-start.22
  525.1 36.7 %copy-start.15 = (f32[1,1024]{1,0:T(1,128)}, f32[1,1024]{1,0:T(1,128)S(1)}, u32[]{:S(2)}) copy-start(f32[1,1024]{1,0:T(1,128)S(1)} %get-tuple-element.34) | copy-start | bytes 12292
  525.1 36.7 %copy-start.17 = (f32[1,1024]{1,0:T(1,128)}, f32[1,1024]{1,0:T(1,128)S(1)}, u32[]{:S(2)}) copy-start(f32[1,1024]{1,0:T(1,128)S(1)} %get-tuple-element.38) | copy-start | bytes 12292
  561.4 1.6 collective-permute-start.23
  562.4 6.6 copy-start.12
  568.6 1.2 collective-permute-start.24
  592.5 13.9 %copy-start.9 = (f32[3,1024]{1,0:T(4,128)S(1)}, f32[3,1024]{1,0:T(4,128)}, u32[]{:S(2)}) copy-start(f32[3,1024]{1,0:T(4,128)} %get-tuple-element.57) | copy-start | bytes 36868
  592.5 13.9 %copy-start.11 = (f32[3,1024]{1,0:T(4,128)S(1)}, f32[3,1024]{1,0:T(4,128)}, u32[]{:S(2)}) copy-start(f32[3,1024]{1,0:T(4,128)} %get-tuple-element.58) | copy-start | bytes 36868
  592.6 13.8 %copy-start.13 = (f32[1,1024]{1,0:T(1,128)S(1)}, f32[1,1024]{1,0:T(1,128)}, u32[]{:S(2)}) copy-start(f32[1,1024]{1,0:T(1,128)} %copy-done.12) | copy-start | bytes 12292
  606.0 1.8 collective-permute-start.25
  607.7 5.9 copy-start.24
  607.7 5.9 copy-start.26
  613.5 1.2 collective-permute-start.26
  650.8 1.6 collective-permute-start.27
  658.1 1.2 collective-permute-start.28
  695.5 1.5 collective-permute-start.29
  (28 other events, 59.2 us)
where the time goes:
time: 710 us; the launch traced here: 702 us
  other arithmetic  482 us (68%)
  local copies, waits for them, and re-layouts  179 us (25%)
  waiting for transfers between devices  25.7 us (4%)
  starting transfers between devices  11.7 us (2%)
    scatter-add x30, other arithmetic, atom_field(): force = jnp.zeros((3, count + halo), jnp.float32).at[:, first].add(weight...  395 us
    gather x24, local copies, waits for them, and re-layouts, solve_bonds(): current = current - scale * inner(unit, field[:, first] - field[:, second])  88.8 us
    scatter-add x15, other arithmetic, atom_field(): own_field = inv_mass * force[:, :count].at[:, left_atoms].add(returned)  54.2 us
    reduce_sum x19, other arithmetic, inner(): return jnp.sum(left * right, axis=0)  27.5 us
    ppermute x30, waiting for transfers between devices, shifted(): return lax.ppermute(value, axis, pairs)  25.7 us
    gather x2, local copies, waits for them, and re-layouts, solve_bonds(): scale = 1.0 / jnp.sqrt(mass_ext[first] + mass_ext[second])  18.2 us
    gather x27, local copies, waits for them, and re-layouts, atom_field(): edge_field = shifted(own_field[:, left_atoms], 'dom', -1)  16.8 us
    gather x4, local copies, waits for them, and re-layouts, solve_bonds(): gap = now[:, first] - now[:, second]  14.8 us
  transfers between devices with their start and end apart: 30, of which 29 were waited for; matrix products, arithmetic and copies ran while one was open for 1% of the time, Pallas kernels for 0%

commit v1 on v0

v1 whole, which is shorter than its diff:
```python
import functools
import math

import jax
import jax.numpy as jnp
from jax import lax
from jax.experimental import pallas as pl
from jax.experimental.pallas import tpu as pltpu
from jax.sharding import PartitionSpec as P

ORDER = 4
ITER = 2
LANES = 128
SUB = 8


time_step = 0.002
mass_oxygen = 15.9994
mass_hydrogen = 1.008
oxygen_hydrogen = 0.09572
hydrogen_pair = 0.15139
total_mass = mass_oxygen + 2.0 * mass_hydrogen
half_pair = 0.5 * hydrogen_pair
water_height = math.sqrt(oxygen_hydrogen * oxygen_hydrogen - half_pair * half_pair)
oxygen_reach = 2.0 * mass_hydrogen * water_height / total_mass
hydrogen_reach = water_height - oxygen_reach


def cross_product(left, right):
    return [
        left[1] * right[2] - left[2] * right[1],
        left[2] * right[0] - left[0] * right[2],
        left[0] * right[1] - left[1] * right[0],
    ]


def inner(left, right):
    return left[0] * right[0] + left[1] * right[1] + left[2] * right[2]


def minus(left, right):
    return [a - b for a, b in zip(left, right)]


def settle(before, after):
    old_oxygen, old_first, old_second = (before[0:3], before[3:6], before[6:9])
    new_oxygen, new_first, new_second = (after[0:3], after[3:6], after[6:9])
    center = [
        (mass_oxygen * o + mass_hydrogen * (f + s)) / total_mass
        for o, f, s in zip(new_oxygen, new_first, new_second)
    ]
    old_b = minus(old_first, old_oxygen)
    old_c = minus(old_second, old_oxygen)
    rel_a = minus(new_oxygen, center)
    rel_b = minus(new_first, center)
    rel_c = minus(new_second, center)
    normal = cross_product(old_b, old_c)
    side = cross_product(rel_a, normal)
    upward = cross_product(normal, side)

    def normed(vector):
        size = jnp.sqrt(inner(vector, vector))
        return [a / size for a in vector]

    axis_z = normed(normal)
    axis_x = normed(side)
    axis_y = normed(upward)
    oldb_x = inner(axis_x, old_b)
    oldb_y = inner(axis_y, old_b)
    oldc_x = inner(axis_x, old_c)
    oldc_y = inner(axis_y, old_c)
    newa_z = inner(axis_z, rel_a)
    newb_x = inner(axis_x, rel_b)
    newb_y = inner(axis_y, rel_b)
    newb_z = inner(axis_z, rel_b)
    newc_x = inner(axis_x, rel_c)
    newc_y = inner(axis_y, rel_c)
    newc_z = inner(axis_z, rel_c)
    sin_phi = newa_z / oxygen_reach
    cos_phi = jnp.sqrt(1.0 - sin_phi * sin_phi)
    sin_psi = (newb_z - newc_z) / (2.0 * half_pair * cos_phi)
    cos_psi = jnp.sqrt(1.0 - sin_psi * sin_psi)
    rest_ay = oxygen_reach * cos_phi
    rest_bx = -half_pair * cos_psi
    lowered = -hydrogen_reach * cos_phi
    tilted = half_pair * sin_psi * sin_phi
    rest_by = lowered - tilted
    rest_cy = lowered + tilted
    alpha = rest_bx * (oldb_x - oldc_x) + oldb_y * rest_by + oldc_y * rest_cy
    beta = rest_bx * (oldc_y - oldb_y) + oldb_x * rest_by + oldc_x * rest_cy
    gamma = oldb_x * newb_y - newb_x * oldb_y + oldc_x * newc_y - newc_x * oldc_y
    summed = alpha * alpha + beta * beta
    sin_theta = (alpha * gamma - beta * jnp.sqrt(summed - gamma * gamma)) / summed
    cos_theta = jnp.sqrt(1.0 - sin_theta * sin_theta)
    final_ax = -rest_ay * sin_theta
    final_ay = rest_ay * cos_theta
    final_bx = rest_bx * cos_theta - rest_by * sin_theta
    final_by = rest_bx * sin_theta + rest_by * cos_theta
    final_cx = -rest_bx * cos_theta - rest_cy * sin_theta
    final_cy = -rest_bx * sin_theta + rest_cy * cos_theta

    def placed(x, y, z):
        return [
            center[c] + axis_x[c] * x + axis_y[c] * y + axis_z[c] * z for c in range(3)
        ]

    return (
        placed(final_ax, final_ay, newa_z)
        + placed(final_bx, final_by, newb_z)
        + placed(final_cx, final_cy, newc_z)
    )


def lane_gather(table, index):
    return jnp.take_along_axis(table, index, axis=1, mode="promise_in_bounds")


def kernel(
    n, axis, pos, vel, mass, bonds, left, right, wpos, wvel, out_p, out_w,
    pos_x, vel_x, mass_x, bonds_x, left_x, right_x,
    first_s, second_s, packed_s, rows_s, lanes_s, lhs_s, field_s, water_s,
    send_sem, recv_sem,
):
    atom_rows = mass.shape[0]
    bond_rows = bonds.shape[1] // LANES
    halo_rows = left.shape[0]
    used = bond_rows + halo_rows
    con_rows = first_s.shape[1]
    tiles = con_rows // SUB
    half_rows = 2 * used
    water_rows = wpos.shape[1] // LANES

    own = (pos, vel, mass, bonds, left, right)
    others = (pos_x, vel_x, mass_x, bonds_x, left_x, right_x)
    me = lax.axis_index(axis)
    copies = []
    if n > 1:
        barrier = pltpu.get_barrier_semaphore()
        for k in range(1, n):
            peer = lax.rem(me + k, n)
            pl.semaphore_signal(
                barrier, inc=1, device_id={axis: peer},
                device_id_type=pl.DeviceIdType.MESH,
            )
        pl.semaphore_wait(barrier, n - 1)
        for k in range(1, n):
            peer = lax.rem(me + n - k, n)
            for t in range(len(own)):
                copy = pltpu.make_async_remote_copy(
                    src_ref=own[t],
                    dst_ref=others[t].at[k - 1],
                    send_sem=send_sem.at[k - 1, t],
                    recv_sem=recv_sem.at[k - 1, t],
                    device_id={axis: peer},
                    device_id_type=pl.DeviceIdType.MESH,
                )
                copy.start()
                copies.append(copy)

    components = wpos.shape[0]
    for source, base in ((wpos, 0), (wvel, components)):
        for c in range(components):
            for r in range(water_rows):
                water_s[base + c, pl.ds(r, 1), :] = source[
                    pl.ds(c, 1), pl.ds(r * LANES, LANES)
                ]
    before = [water_s[c] for c in range(components)]
    speed = [water_s[components + c] for c in range(components)]
    after = [b + time_step * v for b, v in zip(before, speed)]
    settled = settle(before, after)
    for c in range(components):
        water_s[c] = speed[c] + (settled[c] - after[c]) / time_step
    for c in range(components):
        for r in range(water_rows):
            out_w[pl.ds(c, 1), pl.ds(r * LANES, LANES)] = water_s[c, pl.ds(r, 1), :]

    for copy in copies:
        copy.wait()

    def data(k):
        return own if k == 0 else tuple(ref.at[k - 1] for ref in others)

    for k in range(n):
        bonds_k, right_k = data(k)[3], data(k)[5]
        left_k = data((k + 1) % n)[4]
        first_s[k, pl.ds(used, con_rows - used), :] = jnp.zeros(
            (con_rows - used, LANES), jnp.int32
        )
        second_s[k, pl.ds(used, con_rows - used), :] = jnp.zeros(
            (con_rows - used, LANES), jnp.int32
        )
        for r in range(bond_rows):
            first_s[k, pl.ds(r, 1), :] = bonds_k[pl.ds(0, 1), pl.ds(r * LANES, LANES)]
            second_s[k, pl.ds(r, 1), :] = bonds_k[pl.ds(1, 1), pl.ds(r * LANES, LANES)]
        first_s[k, pl.ds(bond_rows, halo_rows), :] = right_k[...]
        second_s[k, pl.ds(bond_rows, halo_rows), :] = left_k[...]

    row_iota = lax.broadcasted_iota(jnp.int32, (atom_rows, LANES), 0)
    lane_iota = lax.broadcasted_iota(jnp.int32, (LANES, LANES), 0)
    half_source = []
    for k in range(n):
        sources = [(k, r, first_s, k, 1.0) for r in range(used)]
        sources += [(k, r, second_s, k, -1.0) for r in range(bond_rows)]
        back = (k + n - 1) % n
        sources += [(back, r, second_s, back, -1.0) for r in range(bond_rows, used)]
        half_source.append([(s[0], s[1]) for s in sources])
        for p, (_, r, ref, slot, sign) in enumerate(sources):
            index = ref[slot, pl.ds(r, 1), :]
            rows_s[k, p] = jnp.where(row_iota == (index >> 7), sign, 0.0).astype(
                jnp.bfloat16
            )
            lanes_s[k, :, pl.ds(p * LANES, LANES)] = jnp.where(
                lane_iota == (index & 127), 1.0, 0.0
            ).astype(jnp.bfloat16)

    position = lax.broadcasted_iota(jnp.int32, (SUB, LANES), 0)
    valid = [position + v * SUB < used for v in range(tiles)]

    def gathered(k, tables):
        following = (k + 1) % n
        firsts = [[None] * tiles for _ in tables]
        seconds = [[None] * tiles for _ in tables]
        for v in range(tiles):
            index_i = first_s[k, pl.ds(v * SUB, SUB), :]
            index_j = second_s[k, pl.ds(v * SUB, SUB), :]
            lane_i, row_i = index_i & 127, index_i >> 7
            lane_j, row_j = index_j & 127, index_j >> 7
            low, high = v * SUB, (v + 1) * SUB
            for r in range(atom_rows):
                hit_i = row_i == r
                hit_j = row_j == r
                for c, table in enumerate(tables):
                    mine = jnp.broadcast_to(table(k, r), (SUB, LANES))
                    if high <= bond_rows:
                        there = mine
                    else:
                        there = jnp.broadcast_to(table(following, r), (SUB, LANES))
                        if low < bond_rows:
                            there = jnp.where(position + low < bond_rows, mine, there)
                    got_i = lane_gather(mine, lane_i)
                    got_j = lane_gather(there, lane_j)
                    if r > 0:
                        got_i = jnp.where(hit_i, got_i, firsts[c][v])
                        got_j = jnp.where(hit_j, got_j, seconds[c][v])
                    firsts[c][v] = got_i
                    seconds[c][v] = got_j
        join = lambda parts: jnp.concatenate(parts, axis=0)
        return [join(f) for f in firsts], [join(s) for s in seconds]

    valid = jnp.concatenate(valid, axis=0)
    unit, length, scale, gap, value = [], [], [], [], []
    for k in range(n):
        tables = []
        for which in (0, 1):
            for c in range(3):
                tables.append(
                    lambda slot, r, which=which, c=c: data(slot)[which][
                        pl.ds(c, 1), pl.ds(r * LANES, LANES)
                    ]
                )
        tables.append(lambda slot, r: data(slot)[2][pl.ds(r, 1), :])
        at_i, at_j = gathered(k, tables)
        diff = minus(at_i[0:3], at_j[0:3])
        size = jnp.where(valid, jnp.sqrt(inner(diff, diff)), 1.0)
        unit.append([d / size for d in diff])
        length.append(size)
        scale.append(jnp.where(valid, 1.0 / jnp.sqrt(at_i[6] + at_j[6]), 0.0))
        moved_i = [p + time_step * q for p, q in zip(at_i[0:3], at_i[3:6])]
        moved_j = [p + time_step * q for p, q in zip(at_j[0:3], at_j[3:6])]
        gap.append(minus(moved_i, moved_j))
        value.append(scale[k] * (inner(unit[k], gap[k]) - length[k]))
    scaled_unit = [[scale[k] * u for u in unit[k]] for k in range(n)]

    def make_field(values, slots):
        for k in range(n):
            for c in range(3):
                weighted = scaled_unit[k][c] * values[k]
                high = weighted.astype(jnp.bfloat16).astype(jnp.float32)
                packed_s[k, c] = high
                packed_s[k, 3 + c] = weighted - high
        for k in slots:
            for p, (slot, r) in enumerate(half_source[k]):
                hot = rows_s[k, p]
                for j in range(6):
                    wide = jnp.broadcast_to(
                        packed_s[slot, j, pl.ds(r, 1), :], (atom_rows, LANES)
                    ).astype(jnp.bfloat16)
                    lhs_s[k, pl.ds(j * atom_rows, atom_rows), pl.ds(p * LANES, LANES)] = (
                        wide * hot
                    )
            summed = lax.dot_general(
                lhs_s[k], lanes_s[k], (((1,), (1,)), ((), ())),
                preferred_element_type=jnp.float32,
            )
            weight = data(k)[2][...]
            for c in range(3):
                field_s[k, c] = weight * (
                    summed[c * atom_rows:(c + 1) * atom_rows]
                    + summed[(3 + c) * atom_rows:(4 + c) * atom_rows]
                )

    field_tables = [
        lambda slot, r, c=c: field_s[slot, c, pl.ds(r, 1), :] for c in range(3)
    ]

    def field_gap(k):
        at_i, at_j = gathered(k, field_tables)
        return minus(at_i, at_j)

    everyone = range(n)

    def one_order(_, carry):
        current, total = carry
        make_field(current, everyone)
        current = [
            current[k] - inner(scaled_unit[k], field_gap(k)) for k in everyone
        ]
        return current, [t + x for t, x in zip(total, current)]

    moved_by = None
    for round_index in range(ITER + 1):
        _, total = lax.fori_loop(0, ORDER, one_order, (value, value))
        last = round_index == ITER
        make_field(total, range(1) if last else everyone)
        own_field = [field_s[0, c] for c in range(3)]
        moved_by = (
            own_field if moved_by is None
            else [m + f for m, f in zip(moved_by, own_field)]
        )
        if not last:
            gap = [minus(gap[k], field_gap(k)) for k in everyone]
            value = []
            for k in everyone:
                target = jnp.sqrt(2.0 * length[k] * length[k] - inner(gap[k], gap[k]))
                value.append(scale[k] * (length[k] - target))
    for c in range(3):
        field_s[0, c] = moved_by[c] / time_step
    for c in range(3):
        for r in range(atom_rows):
            cols = pl.ds(r * LANES, LANES)
            out_p[pl.ds(c, 1), cols] = (
                vel[pl.ds(c, 1), cols] - field_s[0, c, pl.ds(r, 1), :]
            )


def on_device(
    n, protein_pos, protein_vel, inv_mass, bond_atoms, left_atoms, right_atoms, water_pos, water_vel
):
    atoms = protein_pos.shape[1]
    atom_rows = atoms // LANES
    bond_rows = bond_atoms.shape[1] // LANES
    halo_rows = left_atoms.shape[0] // LANES
    con_rows = -(-(bond_rows + halo_rows + 1) // SUB) * SUB
    half = 2 * (bond_rows + halo_rows)
    others = max(n - 1, 1)
    mass = inv_mass.reshape(atom_rows, LANES)
    left = left_atoms.reshape(halo_rows, LANES)
    right = right_atoms.reshape(halo_rows, LANES)
    operands = (protein_pos, protein_vel, mass, bond_atoms, left, right, water_pos, water_vel)
    vmem = pl.BlockSpec(memory_space=pltpu.VMEM)
    return pl.pallas_call(
        functools.partial(kernel, n, "dom"),
        out_shape=(
            jax.ShapeDtypeStruct(protein_vel.shape, jnp.float32),
            jax.ShapeDtypeStruct(water_vel.shape, jnp.float32),
        ),
        in_specs=[vmem] * len(operands),
        out_specs=(vmem, vmem),
        scratch_shapes=[
            pltpu.VMEM((others,) + x.shape, x.dtype) for x in operands[:6]
        ] + [
            pltpu.VMEM((n, con_rows, LANES), jnp.int32),
            pltpu.VMEM((n, con_rows, LANES), jnp.int32),
            pltpu.VMEM((n, 6, con_rows, LANES), jnp.float32),
            pltpu.VMEM((n, half, atom_rows, LANES), jnp.bfloat16),
            pltpu.VMEM((n, LANES, half * LANES), jnp.bfloat16),
            pltpu.VMEM((n, 6 * atom_rows, half * LANES), jnp.bfloat16),
            pltpu.VMEM((n, 3, atom_rows, LANES), jnp.float32),
            pltpu.VMEM((2 * water_pos.shape[0], water_pos.shape[1] // LANES, LANES), jnp.float32),
            pltpu.SemaphoreType.DMA((others, 6)),
            pltpu.SemaphoreType.DMA((others, 6)),
        ],
        compiler_params=pltpu.CompilerParams(
            collective_id=0, has_side_effects=True, vmem_limit_bytes=60 * 1024 * 1024
        ),
    )(*operands)


def solution(mesh):
    in_specs = (
        P(None, ("rep", "dom")),
        P(None, ("rep", "dom")),
        P(("rep", "dom")),
        P(None, ("rep", "dom")),
        P(("rep", "dom")),
        P(("rep", "dom")),
        P(None, ("rep", "dom")),
        P(None, ("rep", "dom")),
    )
    out_specs = (P(None, ("rep", "dom")), P(None, ("rep", "dom")))
    return jax.shard_map(
        functools.partial(on_device, mesh.shape["dom"]),
        mesh=mesh, in_specs=in_specs, out_specs=out_specs, check_vma=False,
    )
```

time: 710 us -> 28 us (0.04); the launches traced: 702 us -> 27.8 us
  other arithmetic: 482 us -> 0 us
  local copies, waits for them, and re-layouts: 179 us -> 2.04 us
  waiting for transfers between devices: 25.7 us -> 0 us
  Pallas kernels: 0 us -> 25.1 us
  starting transfers between devices: 11.7 us -> 0 us
    scatter-add x45 -> x0, other arithmetic: 449 us -> none  [the longest x30 395 us: atom_field(): force = jnp.zeros((3, count + halo), jnp.float32).at[:, first].add(weight...]
    gather x66 -> x0, local copies, waits for them, and re-layouts: 160 us -> none  [the longest x24 88.8 us: solve_bonds(): current = current - scale * inner(unit, field[:, first] - field[:, second])]
    reduce_sum x19 -> x0, other arithmetic: 27.5 us -> none  [inner(): return jnp.sum(left * right, axis=0)]
    ppermute x30 -> x0, waiting for transfers between devices: 25.7 us -> none  [shifted(): return lax.ppermute(value, axis, pairs)]
    pallas_call x0 -> x1, Pallas kernels: none -> 25.1 us  [on_device(): pl.pallas_call(functools.partial(kernel, n, 'dom'), out_shape=(jax.ShapeD...]
    ppermute x30 -> x0, starting transfers between devices: 11.7 us -> none  [shifted(): return lax.ppermute(value, axis, pairs)]
  transfers between devices with their start and end apart: 30 -> 0, of which waited for: 29 -> 0; matrix products, arithmetic and copies ran while one was open for 1% -> 0% of each run, Pallas kernels for 0% -> 0%
where the time goes in v1:
time: 28 us; the launch traced here: 27.8 us
  Pallas kernels  25.1 us (90%)
  local copies, waits for them, and re-layouts  2.04 us (7%)
  between operations  0.65 us (2%)
    pallas_call x1, Pallas kernels, on_device(): pl.pallas_call(functools.partial(kernel, n, 'dom'), out_shape=(jax.ShapeD...  25.1 us
    unnamed x4, local copies, waits for them, and re-layouts  2.04 us

profile of v1, /device:TPU:3, one launch (start us, length us, event | category | flops | bytes accessed | tf_op | source)
XLA Modules:
  0.0 27.8 jit_solution(3032162914387426901)
XLA Ops:
  0.6 25.1 %shard_map.95 = (f32[3,2048]{1,0:T(4,128)}, f32[9,1024]{1,0:T(8,128)}) custom-call(f32[3,2048]{1,0:T(4,128)} %pos.1, f32[3,2048]{1,0:T(4,128)} %vel.1, f32[16,128]{1,0:T(8,128)} %bitcast.3, s32[2,1280]{1,0:T(2,128)} %bonds.1, s32[3,128]{1,0:T(4,128)} %bitcast.4, s32[3,128]{1,0:T(4,128)} %bitcast.5, f32[9,1024]{1,0:T(8,128)} %wpos.1, f32[9,1024]{1,0:T(8,128)} %wvel.1), custom_call_target="tpu_custom_call" | custom-call | tf_op jit(solution)/shard_map/pallas_call | solution.py:361
  25.7 0.0 copy-start
  25.7 1.4 %copy.12 = f32[3,2048]{1,0:T(4,128)} copy(f32[3,2048]{1,0:T(4,128)} %get-tuple-element.4) | data formatting | bytes 49152
  27.2 0.0 copy-done
  27.2 0.6 %copy.13 = f32[9,1024]{1,0:T(8,128)} copy(f32[9,1024]{1,0:T(8,128)S(1)} %copy-done) | data formatting | bytes 73728
Async XLA Ops:
  25.7 1.4 %copy-start = (f32[9,1024]{1,0:T(8,128)S(1)}, f32[9,1024]{1,0:T(8,128)}, u32[]{:S(2)}) copy-start(f32[9,1024]{1,0:T(8,128)} %get-tuple-element.5) | copy-start | bytes 110596

commit v2 on v1

--- a/solution.py
+++ b/solution.py
@@ -174,37 +174,38 @@
         for r in range(water_rows):
             out_w[pl.ds(c, 1), pl.ds(r * LANES, LANES)] = water_s[c, pl.ds(r, 1), :]
 
-    for copy in copies:
-        copy.wait()
-
     def data(k):
         return own if k == 0 else tuple(ref.at[k - 1] for ref in others)
 
-    for k in range(n):
-        bonds_k, right_k = data(k)[3], data(k)[5]
-        left_k = data((k + 1) % n)[4]
-        first_s[k, pl.ds(used, con_rows - used), :] = jnp.zeros(
-            (con_rows - used, LANES), jnp.int32
-        )
-        second_s[k, pl.ds(used, con_rows - used), :] = jnp.zeros(
-            (con_rows - used, LANES), jnp.int32
-        )
+    def index_bonds(k):
+        bonds_k = data(k)[3]
         for r in range(bond_rows):
             first_s[k, pl.ds(r, 1), :] = bonds_k[pl.ds(0, 1), pl.ds(r * LANES, LANES)]
             second_s[k, pl.ds(r, 1), :] = bonds_k[pl.ds(1, 1), pl.ds(r * LANES, LANES)]
-        first_s[k, pl.ds(bond_rows, halo_rows), :] = right_k[...]
-        second_s[k, pl.ds(bond_rows, halo_rows), :] = left_k[...]
+
+    def index_cross(k):
+        blank = jnp.zeros((con_rows - used, LANES), jnp.int32)
+        first_s[k, pl.ds(used, con_rows - used), :] = blank
+        second_s[k, pl.ds(used, con_rows - used), :] = blank
+        first_s[k, pl.ds(bond_rows, halo_rows), :] = data(k)[5][...]
+        second_s[k, pl.ds(bond_rows, halo_rows), :] = data((k + 1) % n)[4][...]
 
     row_iota = lax.broadcasted_iota(jnp.int32, (atom_rows, LANES), 0)
     lane_iota = lax.broadcasted_iota(jnp.int32, (LANES, LANES), 0)
-    half_source = []
+    pure = bond_rows // SUB
+    half_source, half_index = [], []
     for k in range(n):
         sources = [(k, r, first_s, k, 1.0) for r in range(used)]
         sources += [(k, r, second_s, k, -1.0) for r in range(bond_rows)]
         back = (k + n - 1) % n
         sources += [(back, r, second_s, back, -1.0) for r in range(bond_rows, used)]
+        sources.sort(key=lambda item: item[1] >= pure * SUB)
         half_source.append([(s[0], s[1]) for s in sources])
-        for p, (_, r, ref, slot, sign) in enumerate(sources):
+        half_index.append(sources)
+
+    def one_hots(k, chosen):
+        for p in chosen:
+            _, r, ref, slot, sign = half_index[k][p]
             index = ref[slot, pl.ds(r, 1), :]
             rows_s[k, p] = jnp.where(row_iota == (index >> 7), sign, 0.0).astype(
                 jnp.bfloat16
@@ -216,70 +217,92 @@
     position = lax.broadcasted_iota(jnp.int32, (SUB, LANES), 0)
     valid = [position + v * SUB < used for v in range(tiles)]
 
-    def gathered(k, tables):
+    def one_end(k, v, ref, tables):
         following = (k + 1) % n
-        firsts = [[None] * tiles for _ in tables]
-        seconds = [[None] * tiles for _ in tables]
-        for v in range(tiles):
-            index_i = first_s[k, pl.ds(v * SUB, SUB), :]
-            index_j = second_s[k, pl.ds(v * SUB, SUB), :]
-            lane_i, row_i = index_i & 127, index_i >> 7
-            lane_j, row_j = index_j & 127, index_j >> 7
-            low, high = v * SUB, (v + 1) * SUB
-            for r in range(atom_rows):
-                hit_i = row_i == r
-                hit_j = row_j == r
-                for c, table in enumerate(tables):
-                    mine = jnp.broadcast_to(table(k, r), (SUB, LANES))
-                    if high <= bond_rows:
-                        there = mine
-                    else:
-                        there = jnp.broadcast_to(table(following, r), (SUB, LANES))
-                        if low < bond_rows:
-                            there = jnp.where(position + low < bond_rows, mine, there)
-                    got_i = lane_gather(mine, lane_i)
-                    got_j = lane_gather(there, lane_j)
-                    if r > 0:
-                        got_i = jnp.where(hit_i, got_i, firsts[c][v])
-                        got_j = jnp.where(hit_j, got_j, seconds[c][v])
-                    firsts[c][v] = got_i
-                    seconds[c][v] = got_j
-        join = lambda parts: jnp.concatenate(parts, axis=0)
-        return [join(f) for f in firsts], [join(s) for s in seconds]
-
-    valid = jnp.concatenate(valid, axis=0)
-    unit, length, scale, gap, value = [], [], [], [], []
-    for k in range(n):
-        tables = []
-        for which in (0, 1):
-            for c in range(3):
-                tables.append(
-                    lambda slot, r, which=which, c=c: data(slot)[which][
-                        pl.ds(c, 1), pl.ds(r * LANES, LANES)
-                    ]
-                )
-        tables.append(lambda slot, r: data(slot)[2][pl.ds(r, 1), :])
-        at_i, at_j = gathered(k, tables)
+        index = ref[k, pl.ds(v * SUB, SUB), :]
+        lane, row = index & 127, index >> 7
+        low, high = v * SUB, (v + 1) * SUB
+        found = [None] * len(tables)
+        for r in range(atom_rows):
+            hit = row == r
+            for c, table in enumerate(tables):
+                source = jnp.broadcast_to(table(k, r), (SUB, LANES))
+                if ref is second_s and high > bond_rows:
+                    there = jnp.broadcast_to(table(following, r), (SUB, LANES))
+                    if low < bond_rows:
+                        there = jnp.where(position + low < bond_rows, source, there)
+                    source = there
+                got = lane_gather(source, lane)
+                found[c] = got if r == 0 else jnp.where(hit, got, found[c])
+        return found
+
+    unit, length, scale, gap, value = (
+        [[None] * tiles for _ in range(n)] for _ in range(5)
+    )
+    tables = []
+    for which in (0, 1):
+        for c in range(3):
+            tables.append(
+                lambda slot, r, which=which, c=c: data(slot)[which][
+                    pl.ds(c, 1), pl.ds(r * LANES, LANES)
+                ]
+            )
+    tables.append(lambda slot, r: data(slot)[2][pl.ds(r, 1), :])
+
+    def start(k, v):
+        at_i = one_end(k, v, first_s, tables)
+        at_j = one_end(k, v, second_s, tables)
         diff = minus(at_i[0:3], at_j[0:3])
-        size = jnp.where(valid, jnp.sqrt(inner(diff, diff)), 1.0)
-        unit.append([d / size for d in diff])
-        length.append(size)
-        scale.append(jnp.where(valid, 1.0 / jnp.sqrt(at_i[6] + at_j[6]), 0.0))
+        size = jnp.where(valid[v], jnp.sqrt(inner(diff, diff)), 1.0)
         moved_i = [p + time_step * q for p, q in zip(at_i[0:3], at_i[3:6])]
         moved_j = [p + time_step * q for p, q in zip(at_j[0:3], at_j[3:6])]
-        gap.append(minus(moved_i, moved_j))
-        value.append(scale[k] * (inner(unit[k], gap[k]) - length[k]))
-    scaled_unit = [[scale[k] * u for u in unit[k]] for k in range(n)]
-
-    def make_field(values, slots):
-        for k in range(n):
+        unit[k][v] = [d / size for d in diff]
+        length[k][v] = size
+        scale[k][v] = jnp.where(valid[v], 1.0 / jnp.sqrt(at_i[6] + at_j[6]), 0.0)
+        gap[k][v] = minus(moved_i, moved_j)
+        value[k][v] = scale[k][v] * (inner(unit[k][v], gap[k][v]) - size)
+
+    early = 2 * pure * SUB
+    index_bonds(0)
+    one_hots(0, range(early))
+    for v in range(pure):
+        start(0, v)
+    for copy in copies:
+        copy.wait()
+    for k in range(1, n):
+        index_bonds(k)
+    for k in range(n):
+        index_cross(k)
+    one_hots(0, range(early, half_rows))
+    for k in range(1, n):
+        one_hots(k, range(half_rows))
+    for k in range(n):
+        for v in range(tiles):
+            if k > 0 or v >= pure:
+                start(k, v)
+    scaled_unit = [
+        [[scale[k][v] * u for u in unit[k][v]] for v in range(tiles)] for k in range(n)
+    ]
+
+    def pack(values, pairs):
+        for k, v in pairs:
+            rows = pl.ds(v * SUB, SUB)
             for c in range(3):
-                weighted = scaled_unit[k][c] * values[k]
+                weighted = scaled_unit[k][v][c] * values[k][v]
                 high = weighted.astype(jnp.bfloat16).astype(jnp.float32)
-                packed_s[k, c] = high
-                packed_s[k, 3 + c] = weighted - high
-        for k in slots:
-            for p, (slot, r) in enumerate(half_source[k]):
+                packed_s[k, c, rows, :] = high
+                packed_s[k, 3 + c, rows, :] = weighted - high
+
+    cuts = []
+    for low, high in ((0, early), (early, half_rows)):
+        middle = low + (high - low) // 4 * 2
+        cuts += [(a, b) for a, b in ((low, middle), (middle, high)) if b > a]
+
+    def make_field(k):
+        summed = None
+        for low, high in cuts:
+            for p in range(low, high):
+                slot, r = half_source[k][p]
                 hot = rows_s[k, p]
                 for j in range(6):
                     wide = jnp.broadcast_to(
@@ -288,51 +311,80 @@
                     lhs_s[k, pl.ds(j * atom_rows, atom_rows), pl.ds(p * LANES, LANES)] = (
                         wide * hot
                     )
-            summed = lax.dot_general(
-                lhs_s[k], lanes_s[k], (((1,), (1,)), ((), ())),
+            columns = pl.ds(low * LANES, (high - low) * LANES)
+            part = lax.dot_general(
+                lhs_s[k, :, columns], lanes_s[k, :, columns], (((1,), (1,)), ((), ())),
                 preferred_element_type=jnp.float32,
             )
-            weight = data(k)[2][...]
-            for c in range(3):
-                field_s[k, c] = weight * (
-                    summed[c * atom_rows:(c + 1) * atom_rows]
-                    + summed[(3 + c) * atom_rows:(4 + c) * atom_rows]
-                )
+            summed = part if summed is None else summed + part
+        weight = data(k)[2][...]
+        for c in range(3):
+            field_s[k, c] = weight * (
+                summed[c * atom_rows:(c + 1) * atom_rows]
+                + summed[(3 + c) * atom_rows:(4 + c) * atom_rows]
+            )
 
     field_tables = [
         lambda slot, r, c=c: field_s[slot, c, pl.ds(r, 1), :] for c in range(3)
     ]
-
-    def field_gap(k):
-        at_i, at_j = gathered(k, field_tables)
-        return minus(at_i, at_j)
-
-    everyone = range(n)
-
-    def one_order(_, carry):
+    mine = [(0, v) for v in range(tiles)]
+    theirs = [(k, v) for k in range(1, n) for v in range(tiles)]
+    order = (
+        [(0, v) for v in range(pure)]
+        + [(k, v) for k in range(n) for v in range(pure, tiles)]
+        + [(k, v) for k in range(1, n) for v in range(pure)]
+    )
+
+    def other_fields():
+        for k in range(1, n):
+            make_field(k)
+
+    def field_gaps():
+        gaps = [[None] * tiles for _ in range(n)]
+        for k, v in order:
+            at_i = one_end(k, v, first_s, field_tables)
+            at_j = one_end(k, v, second_s, field_tables)
+            gaps[k][v] = minus(at_i, at_j)
+        return gaps
+
+    def over(function, *series):
+        return [
+            [function(*[x[k][v] for x in series]) for v in range(tiles)]
+            for k in range(n)
+        ]
+
+    def one_order(step, carry):
         current, total = carry
-        make_field(current, everyone)
-        current = [
-            current[k] - inner(scaled_unit[k], field_gap(k)) for k in everyone
-        ]
-        return current, [t + x for t, x in zip(total, current)]
-
-    moved_by = None
-    for round_index in range(ITER + 1):
-        _, total = lax.fori_loop(0, ORDER, one_order, (value, value))
-        last = round_index == ITER
-        make_field(total, range(1) if last else everyone)
-        own_field = [field_s[0, c] for c in range(3)]
-        moved_by = (
-            own_field if moved_by is None
-            else [m + f for m, f in zip(moved_by, own_field)]
+        other_fields()
+        current = over(
+            lambda x, su, g: x - inner(su, g), current, scaled_unit, field_gaps()
         )
-        if not last:
-            gap = [minus(gap[k], field_gap(k)) for k in everyone]
-            value = []
-            for k in everyone:
-                target = jnp.sqrt(2.0 * length[k] * length[k] - inner(gap[k], gap[k]))
-                value.append(scale[k] * (length[k] - target))
+        total = over(lambda t, x: t + x, total, current)
+        following = over(lambda x, t: jnp.where(step == ORDER - 1, t, x), current, total)
+        pack(following, mine + theirs)
+        make_field(0)
+        return current, total
+
+    def expand(values):
+        pack(values, mine + theirs)
+        make_field(0)
+        lax.fori_loop(0, ORDER, one_order, (values, values))
+        return [field_s[0, c] for c in range(3)]
+
+    def one_round(_, carry):
+        gap, value, moved_by = carry
+        own_field = expand(value)
+        other_fields()
+        gap = over(minus, gap, field_gaps())
+        value = over(
+            lambda s, l, g: s * (l - jnp.sqrt(2.0 * l * l - inner(g, g))),
+            scale, length, gap,
+        )
+        return gap, value, [m + f for m, f in zip(moved_by, own_field)]
+
+    zero = jnp.zeros((atom_rows, LANES), jnp.float32)
+    gap, value, moved_by = lax.fori_loop(0, ITER, one_round, (gap, value, [zero] * 3))
+    moved_by = [m + f for m, f in zip(moved_by, expand(value))]
     for c in range(3):
         field_s[0, c] = moved_by[c] / time_step
     for c in range(3):

time: 28 us -> 22.9 us (0.82)
  Pallas kernels: 25.1 us -> 20 us
    pallas_call x1, Pallas kernels: 25.1 us -> 20 us  [on_device(): pl.pallas_call(functools.partial(kernel, n, 'dom'), out_shape=(jax.ShapeD...]
where the time goes in v2:
time: 22.9 us; the launch traced here: 22.7 us
  Pallas kernels  20 us (87%)
  local copies, waits for them, and re-layouts  2.04 us (9%)
  between operations  0.65 us (3%)
    pallas_call x1, Pallas kernels, on_device(): pl.pallas_call(functools.partial(kernel, n, 'dom'), out_shape=(jax.ShapeD...  20 us
    unnamed x4, local copies, waits for them, and re-layouts  2.04 us

profile of v2, /device:TPU:3, one launch (start us, length us, event | category | flops | bytes accessed | tf_op | source)
XLA Modules:
  0.0 22.7 jit_solution(15454776100936298994)
XLA Ops:
  0.6 20.0 %shard_map.95 = (f32[3,2048]{1,0:T(4,128)}, f32[9,1024]{1,0:T(8,128)}) custom-call(f32[3,2048]{1,0:T(4,128)} %pos.1, f32[3,2048]{1,0:T(4,128)} %vel.1, f32[16,128]{1,0:T(8,128)} %bitcast.3, s32[2,1280]{1,0:T(2,128)} %bonds.1, s32[3,128]{1,0:T(4,128)} %bitcast.4, s32[3,128]{1,0:T(4,128)} %bitcast.5, f32[9,1024]{1,0:T(8,128)} %wpos.1, f32[9,1024]{1,0:T(8,128)} %wvel.1), custom_call_target="tpu_custom_call" | custom-call | tf_op jit(solution)/shard_map/pallas_call | solution.py:413
  20.6 0.0 copy-start
  20.6 1.4 %copy.12 = f32[3,2048]{1,0:T(4,128)} copy(f32[3,2048]{1,0:T(4,128)} %get-tuple-element.4) | data formatting | bytes 49152
  22.0 0.0 copy-done
  22.0 0.6 %copy.13 = f32[9,1024]{1,0:T(8,128)} copy(f32[9,1024]{1,0:T(8,128)S(1)} %copy-done) | data formatting | bytes 73728
Async XLA Ops:
  20.6 1.4 %copy-start = (f32[9,1024]{1,0:T(8,128)S(1)}, f32[9,1024]{1,0:T(8,128)}, u32[]{:S(2)}) copy-start(f32[9,1024]{1,0:T(8,128)} %get-tuple-element.5) | copy-start | bytes 110596
